TPU v7x, 32 devices: a whole 2x2x4 slice. The times are simulated.
32 devices in a mesh: tm: 4 (over y, x), users: 8 (over z, core).
Axes of the slice: x: 2, y: 2, z: 4, core: 2. Of those that a mesh axis runs over, the one named last changes fastest.
Arguments:
- features: float32 [131072, 128], P(('tm', 'users')), may hold values from -6 to 6
- home: int32 [131072, 1], P(('tm', 'users')), may hold values from 0 to 7; in each aligned block of 4096 rows (0 to 4095, 4096 to 8191, ...) at most 1024 rows name the same one
- account: int32 [131072], P(('tm', 'users')), may hold values from 0 to 127
- flags: int32 [131072], P(('tm', 'users')), may hold values 0 or 1
Outputs:
- session_mean: float32 [131072, 128], P(('tm', 'users'))
Inputs may be any that keep to these rules, and one draw needn't show every extreme that they name: `home`: the 4096 events of one device name one owner at most 1024 times, a bound that some block reaches.
All inputs are finite; a program needn't handle non-finite values. No bound on the sum of `flags` on one device may be relied on, other than what follows from the above.
Results may differ from a plain program's by a relative error of at most 0.00007.
Values sent between devices are 32-bit elements; how exact they have to be, the bound alone decides.
A program may use at most 64 MiB of HBM per device.

v0:
```python
import math

import jax
import jax.numpy as jnp
from jax import lax
from jax.sharding import PartitionSpec as P

ACCOUNTS = 128


EXACT_MATMUL = lax.Precision.HIGHEST


def destination_rank(owner_of, owners):
    count_per_row = owner_of.shape[0]
    block_rows = math.gcd(count_per_row, 512)
    blocks = count_per_row // block_rows
    strict_lower = (
        lax.broadcasted_iota(jnp.int32, (block_rows, block_rows), 0)
        > lax.broadcasted_iota(jnp.int32, (block_rows, block_rows), 1)
    ).astype(jnp.float32)
    columns = jnp.arange(owners, dtype=jnp.int32)

    def destination_advance(before, block_data):
        choose_mask = (block_data[:, None] == columns[None, :]).astype(jnp.float32)
        earlier = jnp.dot(strict_lower, choose_mask, precision=EXACT_MATMUL) + before[None, :]
        return (before + jnp.sum(choose_mask, axis=0), jnp.sum(earlier * choose_mask, axis=1))

    ignored, rank_rows = lax.scan(
        destination_advance, jnp.zeros((owners,), jnp.float32), owner_of.reshape(blocks, block_rows)
    )
    return rank_rows.reshape(count_per_row).astype(jnp.int32)


def decode_rows(code_rows):
    code_ints = code_rows.astype(jnp.int32)
    is_valid = code_ints >= 0
    account_rows = jnp.where(is_valid, code_ints // 2, -1)
    flag_rows = jnp.where(is_valid, code_ints % 2, 0).astype(jnp.float32)
    return (account_rows, flag_rows)


def session_sweep(values, account_rows, flag_rows, accounts):
    count_per_row, feature_count = values.shape
    block_rows = math.gcd(count_per_row, 512)
    blocks = count_per_row // block_rows
    row_ids = lax.broadcasted_iota(jnp.int32, (block_rows, block_rows), 0)
    col_ids = lax.broadcasted_iota(jnp.int32, (block_rows, block_rows), 1)
    up_to = col_ids <= row_ids
    later_rows = col_ids > row_ids
    up_to_float = up_to.astype(jnp.float32)
    columns = jnp.arange(accounts, dtype=jnp.int32)

    def session_advance(carried, block_data):
        open_sum, open_count, already_seen = carried
        rows_values, rows_account, rows_flag = block_data
        is_live = rows_account >= 0
        indicator_matrix = (rows_account[:, None] == columns[None, :]).astype(jnp.float32)
        flag_counts = jnp.dot(
            up_to_float, indicator_matrix * rows_flag[:, None], precision=EXACT_MATMUL
        )
        own_flags = jnp.sum(flag_counts * indicator_matrix, axis=1)
        same_user = (
            (rows_account[:, None] == rows_account[None, :]) & is_live[None, :] & is_live[:, None]
        )
        same_session = (same_user & up_to & (own_flags[:, None] == own_flags[None, :])).astype(
            jnp.float32
        )
        inside_sum = jnp.dot(same_session, rows_values, precision=EXACT_MATMUL)
        inside_count = jnp.sum(same_session, axis=1)
        session_continues = jnp.where(is_live & (own_flags == 0.0), 1.0, 0.0)
        running_sum = inside_sum + session_continues[:, None] * jnp.dot(
            indicator_matrix, open_sum, precision=EXACT_MATMUL
        )
        running_count = inside_count + session_continues * jnp.dot(
            indicator_matrix, open_count, precision=EXACT_MATMUL
        )
        without_flag = session_continues * (
            1.0 - jnp.dot(indicator_matrix, already_seen, precision=EXACT_MATMUL)
        )
        followers = jnp.sum((same_user & later_rows).astype(jnp.float32), axis=1)
        last_weight = jnp.where(is_live & (followers == 0.0), 1.0, 0.0)
        present = jnp.minimum(jnp.sum(indicator_matrix, axis=0), 1.0)
        updated_sum = (
            jnp.einsum(
                "ra,rf->af",
                indicator_matrix,
                last_weight[:, None] * running_sum,
                precision=EXACT_MATMUL,
            )
            + (1.0 - present)[:, None] * open_sum
        )
        updated_count = (
            jnp.dot(last_weight * running_count, indicator_matrix, precision=EXACT_MATMUL)
            + (1.0 - present) * open_count
        )
        any_flag = jnp.minimum(jnp.sum(indicator_matrix * rows_flag[:, None], axis=0), 1.0)
        updated_seen = jnp.maximum(already_seen, any_flag)
        return (
            (updated_sum, updated_count, updated_seen),
            (running_sum, running_count, without_flag),
        )

    start_state = (
        jnp.zeros((accounts, feature_count), jnp.float32),
        jnp.zeros((accounts,), jnp.float32),
        jnp.zeros((accounts,), jnp.float32),
    )
    block_data = (
        values.reshape(blocks, block_rows, feature_count),
        account_rows.reshape(blocks, block_rows),
        flag_rows.reshape(blocks, block_rows),
    )
    closing_state, row_pieces = lax.scan(session_advance, start_state, block_data)
    running_sum = row_pieces[0].reshape(count_per_row, feature_count)
    running_count = row_pieces[1].reshape(count_per_row)
    without_flag = row_pieces[2].reshape(count_per_row)
    return (closing_state, running_sum, running_count, without_flag)


def combine_states(earlier, later):
    carry_on = 1.0 - later[2]
    return (
        later[0] + carry_on[:, None] * earlier[0],
        later[1] + carry_on * earlier[1],
        jnp.maximum(earlier[2], later[2]),
    )


def body(features, home, account, flags):
    owners = lax.axis_size("users")
    event_rows, feature_count = features.shape
    slot_cap = 2 * event_rows // owners
    accounts = ACCOUNTS
    owner_of = home[:, 0]
    rank_rows = destination_rank(owner_of, owners)
    slot_index = owner_of * slot_cap + rank_rows
    code_values = (account * 2 + flags).astype(jnp.float32)
    send_values = (
        jnp.zeros((owners * slot_cap, feature_count), jnp.float32).at[slot_index].set(features)
    )
    send_codes = jnp.full((owners * slot_cap,), -1.0, jnp.float32).at[slot_index].set(code_values)
    got_values, got_codes = (
        lax.all_to_all(
            send_values.reshape(owners, slot_cap, feature_count),
            "users",
            split_axis=0,
            concat_axis=0,
            tiled=True,
        ),
        lax.all_to_all(
            send_codes.reshape(owners, slot_cap), "users", split_axis=0, concat_axis=0, tiled=True
        ),
    )
    account_rows, flag_rows = decode_rows(got_codes.reshape(owners * slot_cap))
    closing_state, running_sum, running_count, without_flag = session_sweep(
        got_values.reshape(owners * slot_cap, feature_count), account_rows, flag_rows, accounts
    )
    identity = (
        jnp.zeros((accounts, feature_count), jnp.float32),
        jnp.zeros((accounts,), jnp.float32),
        jnp.zeros((accounts,), jnp.float32),
    )
    gathered = (
        lax.all_gather(closing_state[0], "tm", axis=0, tiled=True),
        lax.all_gather(closing_state[1], "tm", axis=0, tiled=True),
        lax.all_gather(closing_state[2], "tm", axis=0, tiled=True),
    )
    my_group = lax.axis_index("tm")
    incoming = identity
    for position in range(lax.axis_size("tm")):
        group_state = (
            gathered[0][position * accounts : (position + 1) * accounts],
            gathered[1][position * accounts : (position + 1) * accounts],
            gathered[2][position * accounts : (position + 1) * accounts],
        )
        merged = combine_states(incoming, group_state)
        incoming = (
            jnp.where(position < my_group, merged[0], incoming[0]),
            jnp.where(position < my_group, merged[1], incoming[1]),
            jnp.where(position < my_group, merged[2], incoming[2]),
        )
    columns = jnp.arange(accounts, dtype=jnp.int32)
    onehot_rows = (account_rows[:, None] == columns[None, :]).astype(jnp.float32)
    overall_sum = running_sum + without_flag[:, None] * jnp.dot(
        onehot_rows, incoming[0], precision=EXACT_MATMUL
    )
    overall_count = running_count + without_flag * jnp.dot(
        onehot_rows, incoming[1], precision=EXACT_MATMUL
    )
    session_means = overall_sum / jnp.where(overall_count > 0.0, overall_count, 1.0)[:, None]
    returned_means = lax.all_to_all(
        session_means.reshape(owners, slot_cap, feature_count),
        "users",
        split_axis=0,
        concat_axis=0,
        tiled=True,
    )
    result = returned_means.reshape(owners * slot_cap, feature_count)[slot_index]
    return result


def solution(mesh):
    return jax.shard_map(
        body,
        mesh=mesh,
        in_specs=(
            P(("tm", "users"), None),
            P(("tm", "users"), None),
            P(("tm", "users")),
            P(("tm", "users")),
        ),
        out_specs=P(("tm", "users"), None),
        check_vma=False,
    )
```

profile of v0, /device:TPU:0, one launch (start us, length us, event | category | flops | bytes accessed | tf_op | source)
XLA Modules:
  0.0 385.4 jit_solution(16359685620664613377)
XLA Ops:
  0.6 1.4 reduce.7
  2.1 5.3 %while.34 = (s32[]{:T(128)}, f32[8]{0:T(128)S(1)}, f32[8,512]{1,0:T(8,128)S(1)}, s32[8,512]{1,0:T(8,128)S(1)}, s32[]{:T(128)}, /*index=5*/s32[]{:T(128)}) while((s32[]{:T(128)}, f32[8]{0:T(128)S(1)}, f32[8,512]{1,0:T(8,128)S(1)}, s32[8,512]{1,0:T(8,128)S(1)}, s32[]{:T(128)}, /*index=5*/s32[]{:T(128)}) %tuple.69), condition=%wide.region_3.4_spmd.clone, body=%wide.region_0.3_spmd.clone.sunk | while | flops 25722380 | bytes 14623 | solution.py:29
  8.9 16.1 %scatter_custom_fusion = f32[8192]{0:T(1024)} fusion(s32[4096]{0:T(1024)S(1)} %bitcast.173, f32[4096]{0:T(1024)S(1)} %add_convert_fusion, f32[]{:T(128)} %constant.54.clone.1), kind=kCustom, calls=%fused_computation.134 | custom fusion | bytes 32772 | tf_op jit(solution)/shard_map/scatter | solution.py:142
  25.0 6.4 %all-to-all-start = ((f32[8,1,1024]{2,1,0:T(1,128)}), f32[8,1,1024]{2,1,0:T(1,128)S(1)}, u32[]{:S(2)}, u32[]{:S(2)}) async-start(f32[8,1,1024]{2,1,0:T(1,128)} %bitcast.1), calls=%async_computation | async-start | bytes 65536 | tf_op jit(solution)/shard_map/all_to_all | solution.py:151
  31.3 13.1 %scatter_custom_fusion.1 = f32[8192,128]{1,0:T(8,128)} fusion(s32[4096]{0:T(1024)S(1)} %bitcast.174, f32[4096,128]{1,0:T(8,128)} %param.8, f32[]{:T(128)} %constant.49.clone.1), kind=kCustom, calls=%fused_computation.88 | custom fusion | bytes 4194816 | tf_op jit(solution)/shard_map/scatter | solution.py:140
  44.4 5.1 %all-to-all-start.1 = ((f32[8,1024,128]{2,1,0:T(8,128)}), f32[8,1024,128]{2,1,0:T(8,128)}, u32[]{:S(2)}, u32[]{:S(2)}) async-start(f32[8,1024,128]{2,1,0:T(8,128)} %bitcast.151), calls=%async_computation.1 | async-start | bytes 8388608 | tf_op jit(solution)/shard_map/all_to_all | solution.py:144
  49.8 93.8 %all-to-all-done.1 = f32[8,1024,128]{2,1,0:T(8,128)} async-done(((f32[8,1024,128]{2,1,0:T(8,128)}), f32[8,1024,128]{2,1,0:T(8,128)}, u32[]{:S(2)}, u32[]{:S(2)}) %all-to-all-start.1) | async-done | bytes 4194336 | tf_op jit(solution)/shard_map/all_to_all | solution.py:144
  143.6 90.4 %while.35 = (s32[]{:T(128)}, f32[128,128]{1,0:T(8,128)S(1)}, f32[128]{0:T(128)S(1)}, f32[128]{0:T(128)S(1)}, f32[16,512,128]{2,1,0:T(8,128)}, /*index=5*/f32[16,...) while((s32[]{:T(128)}, f32[128,128]{1,0:T(8,128)S(1)}, ...), condition=%wide.region_12.13_spmd.clone, body=%wide.region_6.12_spmd.clone.sunk | while | flops 1016011008 | bytes 1867940 | solution.py:114
  146.0 1.7 fusion.150
  147.7 1.1 bitcast_dynamic-update-slice_fusion.2
  151.6 1.7 fusion.150
  153.3 1.1 bitcast_dynamic-update-slice_fusion.2
  157.3 1.7 fusion.150
  159.0 1.1 bitcast_dynamic-update-slice_fusion.2
  162.9 1.7 fusion.150
  164.6 1.1 bitcast_dynamic-update-slice_fusion.2
  168.6 1.7 fusion.150
  170.3 1.1 bitcast_dynamic-update-slice_fusion.2
  174.2 1.7 fusion.150
  176.0 1.1 bitcast_dynamic-update-slice_fusion.2
  179.9 1.7 fusion.150
  181.6 1.1 bitcast_dynamic-update-slice_fusion.2
  185.6 1.7 fusion.150
  187.3 1.1 bitcast_dynamic-update-slice_fusion.2
  191.2 1.7 fusion.150
  192.9 1.1 bitcast_dynamic-update-slice_fusion.2
  196.9 1.7 fusion.150
  198.6 1.1 bitcast_dynamic-update-slice_fusion.2
  202.5 1.7 fusion.150
  204.2 1.1 bitcast_dynamic-update-slice_fusion.2
  208.2 1.7 fusion.150
  209.9 1.1 bitcast_dynamic-update-slice_fusion.2
  213.8 1.7 fusion.150
  215.5 1.1 bitcast_dynamic-update-slice_fusion.2
  219.5 1.7 fusion.150
  221.2 1.1 bitcast_dynamic-update-slice_fusion.2
  225.1 1.7 fusion.150
  226.8 1.1 bitcast_dynamic-update-slice_fusion.2
  230.8 1.7 fusion.150
  232.5 1.1 bitcast_dynamic-update-slice_fusion.2
  234.0 8.0 %all-gather = f32[4,1,128]{2,1,0:T(1,128)S(1)} all-gather(f32[1,1,128]{2,1,0:T(1,128)S(1)} %bitcast.184), channel_id=1, replica_groups=mesh['tm'=4,'users'=8] {'tm'}, dimensions={0}, use_global_device_ids=true | all-gather | bytes 2560 | tf_op jit(solution)/shard_map/all_gather | solution.py:167
  242.0 7.9 %all-gather.1 = f32[4,1,128]{2,1,0:T(1,128)S(1)} all-gather(f32[1,1,128]{2,1,0:T(1,128)S(1)} %bitcast.185), channel_id=1, replica_groups=mesh['tm'=4,'users'=8] {'tm'}, dimensions={0}, use_global_device_ids=true | all-gather | bytes 2560 | tf_op jit(solution)/shard_map/all_gather | solution.py:166
  249.9 8.0 %all_gather.9 = f32[512,128]{1,0:T(8,128)S(1)} all-gather(f32[128,128]{1,0:T(8,128)S(1)} %get-tuple-element.117), channel_id=1, replica_groups=mesh['tm'=4,'users'=8] {'tm'}, dimensions={0}, use_global_device_ids=true | all-gather | bytes 327680 | tf_op jit(solution)/shard_map/all_gather | solution.py:165
  257.9 2.9 fusion.58
  260.9 9.6 %fusion.57 = f32[8192,128]{1,0:T(8,128)} fusion(f32[8192,128]{1,0:T(8,128)} %bitcast.186, f32[8192]{0:T(1024)S(1)} %compare_select_fusion.1, s32[8192]{0:T(1024)S(1)} %fusion.78, f32[8192]{0:T(1024)S(1)} %bitcast.171, f32[512,128]{1,0:T(8,128)S(1)} %all_gather.9, f32[128]{0:T(128)S(1)} %get-tuple-element.232, f32[128]{0:T(128)S(1)} %get-tuple-element.230, ...), kind=kOutput, calls=%fused_computation.83 | convolution fusion | flops 1614987264 | bytes 8751108 | tf_op jit(solution)/shard_map/dot_general | solution.py:185
  270.5 4.5 %all-to-all-start.2 = ((f32[8,1024,128]{2,1,0:T(8,128)}), f32[8,1024,128]{2,1,0:T(8,128)}, u32[]{:S(2)}, u32[]{:S(2)}) async-start(f32[8,1024,128]{2,1,0:T(8,128)} %bitcast.152), calls=%async_computation.2 | async-start | bytes 8388608 | tf_op jit(solution)/shard_map/all_to_all | solution.py:192
  275.1 94.0 %all-to-all-done.2 = f32[8,1024,128]{2,1,0:T(8,128)} async-done(((f32[8,1024,128]{2,1,0:T(8,128)}), f32[8,1024,128]{2,1,0:T(8,128)}, u32[]{:S(2)}, u32[]{:S(2)}) %all-to-all-start.2) | async-done | bytes 4194336 | tf_op jit(solution)/shard_map/all_to_all | solution.py:192
  369.0 16.4 %gather_fusion = f32[4096,128]{1,0:T(8,128)} fusion(f32[8192,128]{1,0:T(8,128)} %bitcast.19, s32[4096]{0:T(1024)S(1)} %broadcast_clamp_fusion), kind=kCustom, calls=%fused_computation | custom fusion | bytes 4210688 | tf_op jit(solution)/shard_map/gather | solution.py:199
  (289 shorter events, 51.4 us)
Async XLA Ops:
  25.0 19.5 %all-to-all-start = ((f32[8,1,1024]{2,1,0:T(1,128)}), f32[8,1,1024]{2,1,0:T(1,128)S(1)}, u32[]{:S(2)}, u32[]{:S(2)}) async-start(f32[8,1,1024]{2,1,0:T(1,128)} %bitcast.1), calls=%async_computation | async-start | bytes 65536 | tf_op jit(solution)/shard_map/all_to_all | solution.py:151
  44.4 99.2 %all-to-all-start.1 = ((f32[8,1024,128]{2,1,0:T(8,128)}), f32[8,1024,128]{2,1,0:T(8,128)}, u32[]{:S(2)}, u32[]{:S(2)}) async-start(f32[8,1024,128]{2,1,0:T(8,128)} %bitcast.151), calls=%async_computation.1 | async-start | bytes 8388608 | tf_op jit(solution)/shard_map/all_to_all | solution.py:144
  270.5 98.5 %all-to-all-start.2 = ((f32[8,1024,128]{2,1,0:T(8,128)}), f32[8,1024,128]{2,1,0:T(8,128)}, u32[]{:S(2)}, u32[]{:S(2)}) async-start(f32[8,1024,128]{2,1,0:T(8,128)} %bitcast.152), calls=%async_computation.2 | async-start | bytes 8388608 | tf_op jit(solution)/shard_map/all_to_all | solution.py:192
where the time goes:
time: 387 us; the launch traced here: 385 us
  waiting for transfers between devices  188 us (49%)
  matrix products  90.2 us (23%)
  local copies, waits for them, and re-layouts  49.7 us (13%)
  blocking collectives  23.9 us (6%)
  other arithmetic  16.1 us (4%)
  starting transfers between devices  16 us (4%)
    all_to_all x1, waiting for transfers between devices, body(): lax.all_to_all(session_means.reshape(owners, slot_cap, feature_count), 'u...  94 us
    all_to_all x1, waiting for transfers between devices, body(): lax.all_to_all(send_values.reshape(owners, slot_cap, feature_count), 'use...  93.8 us
    dot_general x16, matrix products, session_advance(): inside_sum = jnp.dot(same_session, rows_values, precision=EXACT_MATMUL)  27.3 us
    dot_general x16, matrix products, session_advance(): jnp.dot(indicator_matrix, open_sum, precision=EXACT_MATMUL)  17.8 us
    gather x1, local copies, waits for them, and re-layouts, body(): returned_means.reshape(owners * slot_cap, feature_count)[slot_index]  16.4 us
    scatter x1, local copies, waits for them, and re-layouts, body(): jnp.full((owners * slot_cap,), -1.0, jnp.float32).at[slot_index]  16.1 us
    dot_general x16, matrix products, session_advance(): jnp.dot(up_to_float, indicator_matrix * rows_flag[:, None], precision=EXA...  14.1 us
    scatter x1, local copies, waits for them, and re-layouts, body(): jnp.zeros((owners * slot_cap, feature_count), jnp.float32).at[slot_index]  13.1 us
  transfers between devices with their start and end apart: 3, of which 2 were waited for; matrix products, arithmetic and copies ran while one was open for 3% of the time, Pallas kernels for 0%

commit v1 on v0

v1 whole, which is shorter than its diff:
```python
import functools
import math

import jax
import jax.numpy as jnp
from jax import lax
from jax.experimental import pallas as pl
from jax.experimental.pallas import tpu as pltpu
from jax.sharding import PartitionSpec as P

ACCOUNTS = 128
LANES = 128
TILE = ACCOUNTS + 8
VMEM_LIMIT = 60 * 1024 * 1024


def column_of(row):
    return jnp.transpose(jnp.broadcast_to(row, (LANES, LANES)))


def row_of(column):
    return jnp.transpose(column)[0:1, :]


def lane_ids(first):
    return lax.broadcasted_iota(jnp.int32, (1, LANES), 1) + first


def lane_slice(start):
    return pl.ds(pl.multiple_of(start, LANES), LANES)


def split_store(ref, rows, values):
    high = values.astype(jnp.bfloat16)
    ref[rows, 0:LANES] = high
    ref[rows, LANES : 2 * LANES] = (values - high.astype(jnp.float32)).astype(jnp.bfloat16)


def closing_states(user_ref, flag_ref, feature_ref, state_ref, halves_ref, mask_ref, fpos_ref):
    events = feature_ref.shape[0]
    chunks = events // LANES
    group = mask_ref.shape[0]
    users = state_ref.shape[1] * 2 * ACCOUNTS
    step = 4

    for chunk in range(chunks):
        at = slice(chunk * LANES, (chunk + 1) * LANES)
        fpos_ref[0:1, at] = jnp.where(flag_ref[0:1, at] > 0, lane_ids(chunk * LANES + 1), 0)

    @pl.loop(0, chunks)
    def _(chunk):
        at = lane_slice(chunk * LANES)
        split_store(halves_ref, at, feature_ref[at, :])

    @pl.loop(0, users // group)
    def _(block):
        @pl.loop(0, group // ACCOUNTS)
        def _(part):
            owner = block * (group // ACCOUNTS) + part
            ids = lax.broadcasted_iota(jnp.int32, (ACCOUNTS, LANES), 0) + owner * ACCOUNTS

            def latest(trip, found):
                for inner in range(step):
                    at = lane_slice((trip * step + inner) * LANES)
                    found = jnp.maximum(
                        found, jnp.where(user_ref[0:1, at] == ids, fpos_ref[0:1, at], 0)
                    )
                return found

            found = lax.fori_loop(
                0, chunks // step, latest, jnp.zeros((ACCOUNTS, LANES), jnp.int32)
            )
            last = jnp.broadcast_to(jnp.max(found, axis=1, keepdims=True), (ACCOUNTS, LANES))
            rows = lane_slice(part * ACCOUNTS)

            def build(trip, count):
                for inner in range(step):
                    first = (trip * step + inner) * LANES
                    at = lane_slice(first)
                    inside = (user_ref[0:1, at] == ids) & (lane_ids(first + 1) >= last)
                    weight = jnp.where(inside, 1.0, 0.0)
                    mask_ref[rows, at] = weight.astype(jnp.bfloat16)
                    count = count + weight
                return count

            count = lax.fori_loop(
                0, chunks // step, build, jnp.zeros((ACCOUNTS, LANES), jnp.float32)
            )
            count = jnp.broadcast_to(jnp.sum(count, axis=1, keepdims=True), (ACCOUNTS, LANES))
            marks = jnp.where(last > 0, 1.0, 0.0)
            stats = jnp.concatenate(
                [row_of(count), row_of(marks), jnp.zeros((6, LANES), jnp.float32)], axis=0
            )
            state_ref[lax.rem(owner, 2), owner // 2, ACCOUNTS:TILE, :] = stats

        total = jnp.dot(mask_ref[...], halves_ref[...], preferred_element_type=jnp.float32)
        total = total[:, 0:LANES] + total[:, LANES : 2 * LANES]
        for part in range(group // ACCOUNTS):
            owner = block * (group // ACCOUNTS) + part
            state_ref[lax.rem(owner, 2), owner // 2, 0:ACCOUNTS, :] = total[
                part * ACCOUNTS : (part + 1) * ACCOUNTS
            ]


def inside_sessions(
    user_ref, fpos_ref, halves_ref, sum_ref, count_ref, open_ref, key_ref, mask_ref, keycol_ref, cnt_ref, acc_ref
):
    events = halves_ref.shape[0]
    rows = mask_ref.shape[0]
    parts = rows // LANES
    diagonal = lax.broadcasted_iota(jnp.int32, (LANES, LANES), 1) <= lax.broadcasted_iota(
        jnp.int32, (LANES, LANES), 0
    )

    @pl.loop(0, events // rows)
    def _(block):
        base = block * rows
        for part in range(parts):
            mine = lane_slice(base + part * LANES)
            ids = column_of(user_ref[0:1, mine])

            def latest(trip, found):
                for inner in range(parts):
                    at = lane_slice(trip * rows + inner * LANES)
                    found = jnp.maximum(
                        found, jnp.where(user_ref[0:1, at] == ids, fpos_ref[0:1, at], 0)
                    )
                return found

            found = lax.fori_loop(0, block, latest, jnp.zeros((LANES, LANES), jnp.int32))
            for inner in range(part + 1):
                at = lane_slice(base + inner * LANES)
                same = user_ref[0:1, at] == ids
                if inner == part:
                    same = same & diagonal
                found = jnp.maximum(found, jnp.where(same, fpos_ref[0:1, at], 0))
            start = jnp.broadcast_to(jnp.max(found, axis=1, keepdims=True), (LANES, LANES))
            key = jnp.where(start > 0, start, -1 - ids)
            keycol_ref[part * LANES : (part + 1) * LANES, :] = key
            key_ref[0:1, mine] = row_of(key)
            open_ref[0:1, mine] = row_of(jnp.where(start > 0, -1, ids))

        for part in range(parts):
            here = slice(part * LANES, (part + 1) * LANES)
            key = keycol_ref[here, :]
            count = jnp.zeros((LANES, LANES), jnp.float32)
            for inner in range(parts):
                to = slice(inner * LANES, (inner + 1) * LANES)
                if inner > part:
                    mask_ref[here, to] = jnp.zeros((LANES, LANES), jnp.bfloat16)
                    continue
                same = key_ref[0:1, lane_slice(base + inner * LANES)] == key
                if inner == part:
                    same = same & diagonal
                weight = jnp.where(same, 1.0, 0.0)
                mask_ref[here, to] = weight.astype(jnp.bfloat16)
                count = count + weight
            cnt_ref[here, :] = count
        acc_ref[...] = jnp.dot(
            mask_ref[...],
            halves_ref[pl.ds(pl.multiple_of(base, rows), rows), :],
            preferred_element_type=jnp.float32,
        )

        @pl.loop(0, block)
        def _(trip):
            for part in range(parts):
                here = slice(part * LANES, (part + 1) * LANES)
                key = keycol_ref[here, :]
                count = cnt_ref[here, :]
                for inner in range(parts):
                    to = slice(inner * LANES, (inner + 1) * LANES)
                    weight = jnp.where(
                        key_ref[0:1, lane_slice(trip * rows + inner * LANES)] == key, 1.0, 0.0
                    )
                    mask_ref[here, to] = weight.astype(jnp.bfloat16)
                    count = count + weight
                cnt_ref[here, :] = count
            acc_ref[...] += jnp.dot(
                mask_ref[...],
                halves_ref[pl.ds(pl.multiple_of(trip * rows, rows), rows), :],
                preferred_element_type=jnp.float32,
            )

        sum_ref[pl.ds(pl.multiple_of(base, rows), rows), :] = (
            acc_ref[:, 0:LANES] + acc_ref[:, LANES : 2 * LANES]
        )
        for part in range(parts):
            here = slice(part * LANES, (part + 1) * LANES)
            count = jnp.sum(cnt_ref[here, :], axis=1, keepdims=True)
            count_ref[0:1, lane_slice(base + part * LANES)] = row_of(
                jnp.broadcast_to(count, (LANES, LANES))
            )


def sums_of(tile):
    return tile[0:ACCOUNTS, :]


def stats_of(tile):
    return tile[ACCOUNTS:TILE, :]


def follow(earlier, later):
    stats_e, stats_l = stats_of(earlier), stats_of(later)
    mark = stats_l[1:2, :]
    carry_on = 1.0 - mark
    sums = sums_of(later) + column_of(carry_on) * sums_of(earlier)
    count = stats_l[0:1, :] + carry_on * stats_e[0:1, :]
    seen = jnp.maximum(mark, stats_e[1:2, :])
    return jnp.concatenate([sums, count, seen, stats_l[2:8, :]], axis=0)


def exchange(
    groups, owners, state_ref, table_ref, count_ref,
    pair_in, chip, chip_in, time_out, time_in, back_out, back_in, pair_out, pair_back, sends, recvs,
):
    chips = owners // 2
    time, me = lax.axis_index("tm"), lax.axis_index("users")
    core, z = lax.rem(me, 2), me // 2
    sibling = me + 1 - 2 * core
    other = 1 - core
    zeros = jnp.zeros((TILE, LANES), jnp.float32)

    def copy(source, target, stage, mine, theirs, device):
        return pltpu.make_async_remote_copy(
            src_ref=source,
            dst_ref=target,
            send_sem=sends.at[stage, mine],
            recv_sem=recvs.at[stage, theirs],
            device_id=device,
            device_id_type=pl.DeviceIdType.MESH,
        )

    def peer(shift):
        return lax.rem(z + shift, chips)

    def each(first, last, fn):
        if last - first <= 8:
            for index in range(first, last):
                fn(index)
        else:
            pl.loop(first, last)(fn)

    def device(group, user):
        return (group, user)

    barrier = pltpu.get_barrier_semaphore()
    pl.semaphore_signal(barrier, inc=1, device_id=device(time, sibling), device_id_type=pl.DeviceIdType.MESH)
    each(1, chips, lambda k: pl.semaphore_signal(
        barrier, inc=1, device_id=device(time, 2 * peer(k) + core), device_id_type=pl.DeviceIdType.MESH))
    each(1, groups, lambda k: pl.semaphore_signal(
        barrier, inc=1, device_id=device(lax.rem(time + k, groups), me), device_id_type=pl.DeviceIdType.MESH))
    pl.semaphore_wait(barrier, 1 + (chips - 1) + (groups - 1))

    def swap(k):
        to = peer(k)
        copy(state_ref.at[other, to], pair_in.at[to], 0, to, to, device(time, sibling)).start()

    each(1, chips, swap)
    swap(0)

    def gather(k):
        to = peer(k)
        got = copy(state_ref.at[other, to], pair_in.at[to], 0, to, to, device(time, sibling))
        got.wait_recv()
        mine, theirs = state_ref[core, to], pair_in[to]
        first = core == 0
        chip[to] = follow(jnp.where(first, mine, theirs), jnp.where(first, theirs, mine))

    def to_owner(k):
        to = peer(k)
        return copy(chip.at[to], chip_in.at[z], 1, to, z, device(time, 2 * to + core))

    def gather_send(k):
        gather(k)
        to_owner(k).start()

    each(1, chips, gather_send)
    gather(0)
    chip_in[z] = chip[z]

    def from_owner(k):
        source = peer(k)
        copy(chip.at[source], chip_in.at[source], 1, source, source, device(time, 2 * source + core)).wait_recv()

    each(1, chips, from_owner)

    total = lax.fori_loop(0, chips, lambda at, so_far: follow(so_far, chip_in[at]), zeros)
    time_out[...] = total

    def to_time(k):
        to = lax.rem(time + k, groups)
        return copy(time_out, time_in.at[time], 2, to, time, device(to, me))

    each(1, groups, lambda k: to_time(k).start())
    time_in[time] = zeros

    def from_time(k):
        source = lax.rem(time + k, groups)
        copy(time_out, time_in.at[source], 2, source, source, device(source, me)).wait_recv()

    each(1, groups, from_time)

    def advance(at, so_far):
        return jnp.where(at < time, follow(so_far, time_in[at]), so_far)

    incoming = lax.fori_loop(0, groups, advance, zeros)

    def prefixes(at, so_far):
        back_out[at] = so_far
        return follow(so_far, chip_in[at])

    lax.fori_loop(0, chips, prefixes, incoming)

    def to_chip(k):
        to = peer(k)
        return copy(back_out.at[to], back_in.at[z], 3, to, z, device(time, 2 * to + core))

    each(1, chips, lambda k: to_chip(k).start())
    back_in[z] = back_out[z]

    def finish(half, at, tile):
        owner = 2 * at + half
        split_store(table_ref, lane_slice(owner * ACCOUNTS), sums_of(tile))
        count_ref[0:1, lane_slice(owner * ACCOUNTS)] = stats_of(tile)[0:1, :]

    def to_sibling(at):
        return copy(pair_out.at[at], pair_back.at[at], 4, at, at, device(time, sibling))

    def hand_over(k):
        at = peer(k)
        tile = back_in[at]
        first = core == 0
        after = follow(tile, jnp.where(first, state_ref[core, at], pair_in[at]))
        pair_out[at] = jnp.where(first, after, tile)
        to_sibling(at).start()
        finish(core, at, jnp.where(first, tile, after))

    def wait_hand_over(k):
        source = peer(k)
        copy(back_out.at[source], back_in.at[source], 3, source, source, device(time, 2 * source + core)).wait_recv()
        hand_over(k)

    hand_over(0)
    each(1, chips, wait_hand_over)

    def last(k):
        at = peer(k)
        to_sibling(at).wait_recv()
        finish(other, at, pair_back[at])

    each(0, chips, last)

    def drain(k):
        to = peer(k)
        to_owner(k).wait_send()
        to_chip(k).wait_send()

    def drain_pair(k):
        to = peer(k)
        copy(state_ref.at[other, to], pair_in.at[to], 0, to, to, device(time, sibling)).wait_send()
        to_sibling(to).wait_send()

    each(1, chips, drain)
    each(0, chips, drain_pair)
    each(1, groups, lambda k: to_time(k).wait_send())


def means(open_ref, own_ref, sum_ref, table_ref, count_ref, out_ref, mask_ref):
    rows, users = mask_ref.shape
    counts = []
    for part in range(rows // LANES):
        here = slice(part * LANES, (part + 1) * LANES)
        ids = column_of(open_ref[0:1, here])

        def build(chunk, count):
            at = lane_slice(chunk * LANES)
            same = lane_ids(chunk * LANES) == ids
            mask_ref[here, at] = jnp.where(same, 1.0, 0.0).astype(jnp.bfloat16)
            return count + jnp.where(same, count_ref[0:1, at], 0.0)

        count = lax.fori_loop(
            0, users // LANES, build, jnp.zeros((LANES, LANES), jnp.float32), unroll=users <= 1024
        )
        counts.append(jnp.sum(count, axis=1, keepdims=True) + column_of(own_ref[0:1, here]))
    before = jnp.dot(mask_ref[...], table_ref[...], preferred_element_type=jnp.float32)
    before = before[:, 0:LANES] + before[:, LANES : 2 * LANES]
    out_ref[...] = (sum_ref[...] + before) / jnp.concatenate(counts, axis=0)


def local_kernel(user_ref, flag_ref, feature_ref, state_ref, sum_ref, count_ref, open_ref,
                 halves, fpos, mask, key, mask2, keycol, cnt, acc):
    closing_states(user_ref, flag_ref, feature_ref, state_ref, halves, mask, fpos)
    inside_sessions(user_ref, fpos, halves, sum_ref, count_ref, open_ref, key, mask2, keycol, cnt, acc)


def body(groups, owners, features, home, account, flags):
    events = features.shape[0]
    users = owners * ACCOUNTS
    chips = owners // 2
    rows = math.gcd(events, 512)
    group = math.gcd(users, 512)
    whole = pl.BlockSpec(memory_space=pltpu.VMEM)
    user = home.reshape(1, events) * ACCOUNTS + account.reshape(1, events)

    state, own_sum, own_count, open_user = pl.pallas_call(
        local_kernel,
        out_shape=(
            jax.ShapeDtypeStruct((2, chips, TILE, LANES), jnp.float32),
            jax.ShapeDtypeStruct((events, LANES), jnp.float32),
            jax.ShapeDtypeStruct((1, events), jnp.float32),
            jax.ShapeDtypeStruct((1, events), jnp.int32),
        ),
        in_specs=[whole] * 3,
        out_specs=(whole,) * 4,
        scratch_shapes=[
            pltpu.VMEM((events, 2 * LANES), jnp.bfloat16),
            pltpu.VMEM((1, events), jnp.int32),
            pltpu.VMEM((group, events), jnp.bfloat16),
            pltpu.VMEM((1, events), jnp.int32),
            pltpu.VMEM((rows, rows), jnp.bfloat16),
            pltpu.VMEM((rows, LANES), jnp.int32),
            pltpu.VMEM((rows, LANES), jnp.float32),
            pltpu.VMEM((rows, 2 * LANES), jnp.float32),
        ],
        compiler_params=pltpu.CompilerParams(vmem_limit_bytes=VMEM_LIMIT),
        name="local",
    )(user, flags.reshape(1, events), features)

    tiles = lambda count: pltpu.VMEM((count, TILE, LANES), jnp.float32)
    lots = max(chips, groups)
    table, prefix_count = pl.pallas_call(
        functools.partial(exchange, groups, owners),
        out_shape=(
            jax.ShapeDtypeStruct((users, 2 * LANES), jnp.bfloat16),
            jax.ShapeDtypeStruct((1, users), jnp.float32),
        ),
        in_specs=[whole],
        out_specs=(whole,) * 2,
        scratch_shapes=[
            tiles(chips), tiles(chips), tiles(chips),
            pltpu.VMEM((TILE, LANES), jnp.float32), tiles(groups),
            tiles(chips), tiles(chips), tiles(chips), tiles(chips),
            pltpu.SemaphoreType.DMA((5, lots)),
            pltpu.SemaphoreType.DMA((5, lots)),
        ],
        compiler_params=pltpu.CompilerParams(
            collective_id=0, has_side_effects=True, vmem_limit_bytes=VMEM_LIMIT
        ),
        name="exchange",
    )(state)

    return pl.pallas_call(
        means,
        grid=(events // rows,),
        out_shape=jax.ShapeDtypeStruct((events, LANES), jnp.float32),
        in_specs=[
            pl.BlockSpec((1, rows), lambda i: (0, i)),
            pl.BlockSpec((1, rows), lambda i: (0, i)),
            pl.BlockSpec((rows, LANES), lambda i: (i, 0)),
            pl.BlockSpec((users, 2 * LANES), lambda i: (0, 0)),
            pl.BlockSpec((1, users), lambda i: (0, 0)),
        ],
        out_specs=pl.BlockSpec((rows, LANES), lambda i: (i, 0)),
        scratch_shapes=[pltpu.VMEM((rows, users), jnp.bfloat16)],
        compiler_params=pltpu.CompilerParams(vmem_limit_bytes=VMEM_LIMIT),
        name="means",
    )(open_user, own_count, own_sum, table, prefix_count)


def solution(mesh):
    return jax.shard_map(
        functools.partial(body, mesh.shape["tm"], mesh.shape["users"]),
        mesh=mesh,
        in_specs=(
            P(("tm", "users"), None),
            P(("tm", "users"), None),
            P(("tm", "users")),
            P(("tm", "users")),
        ),
        out_specs=P(("tm", "users"), None),
        check_vma=False,
    )
```

time: 387 us -> 83.1 us (0.21)
  waiting for transfers between devices: 188 us -> 0 us
  matrix products: 90.2 us -> 0 us
  Pallas kernels: 0 us -> 80.6 us
  local copies, waits for them, and re-layouts: 49.7 us -> 0 us
  blocking collectives: 23.9 us -> 0 us
  starting transfers between devices: 16 us -> 0 us
  other arithmetic: 16.1 us -> 2.05 us
    all_to_all x3 -> x0, waiting for transfers between devices: 188 us -> none  [the longest x1 94 us: body(): lax.all_to_all(session_means.reshape(owners, slot_cap, feature_count), 'u...]
    dot_general x122 -> x0, matrix products: 90.2 us -> none  [the longest x16 27.3 us: session_advance(): inside_sum = jnp.dot(same_session, rows_values, precision=EXACT_MATMUL)]
    pallas_call x0 -> x3, Pallas kernels: none -> 80.6 us  [the longest x1 42.9 us: body(): pl.pallas_call(local_kernel, out_shape=(jax.ShapeDtypeStruct((2, chips, T...]
    scatter x2 -> x0, local copies, waits for them, and re-layouts: 29.2 us -> none  [the longest x1 16.1 us: body(): jnp.full((owners * slot_cap,), -1.0, jnp.float32).at[slot_index]]
    all_gather x3 -> x0, blocking collectives: 23.9 us -> none  [the longest x1 8.02 us: body(): lax.all_gather(closing_state[0], 'tm', axis=0, tiled=True)]
    gather x1 -> x0, local copies, waits for them, and re-layouts: 16.4 us -> none  [body(): returned_means.reshape(owners * slot_cap, feature_count)[slot_index]]
    all_to_all x3 -> x0, starting transfers between devices: 16 us -> none  [the longest x1 6.35 us: body(): lax.all_to_all(send_codes.reshape(owners, slot_cap), 'users', split_axis=...]
    reduce_sum x40 -> x0, other arithmetic: 11.8 us -> none  [the longest x16 8.9 us: session_advance(): inside_count = jnp.sum(same_session, axis=1)]
  transfers between devices with their start and end apart: 3 -> 0, of which waited for: 2 -> 0; matrix products, arithmetic and copies ran while one was open for 3% -> 0% of each run, Pallas kernels for 0% -> 0%
where the time goes in v1:
time: 83.1 us; the launch traced here: 82.7 us
  Pallas kernels  80.6 us (97%)
  other arithmetic  2.05 us (2%)
    pallas_call x1, Pallas kernels, body(): pl.pallas_call(local_kernel, out_shape=(jax.ShapeDtypeStruct((2, chips, T...  42.9 us
    pallas_call x1, Pallas kernels, body(): pl.pallas_call(functools.partial(exchange, groups, owners), out_shape=(ja...  28.5 us
    pallas_call x1, Pallas kernels, body(): pl.pallas_call(means, grid=(events // rows,), out_shape=jax.ShapeDtypeStr...  9.16 us

profile of v1, /device:TPU:0, one launch (start us, length us, event | category | flops | bytes accessed | tf_op | source)
XLA Modules:
  0.0 82.7 jit_solution(13022672530322412676)
XLA Ops:
  0.0 0.7 broadcast_multiply_fusion
  0.7 1.3 %add.5 = s32[4096]{0:T(1024)} add(s32[4096]{0:T(1024)S(1)} %bitcast.4, s32[4096]{0:T(1024)} %param.6) | non-fusion elementwise | flops 4096 | bytes 49152 | tf_op jit(solution)/shard_map/add | solution.py:405
  2.1 42.9 %local.1 = (f32[2,4,136,128]{3,2,1,0:T(8,128)}, f32[4096,128]{1,0:T(8,128)}, f32[1,4096]{1,0:T(1,128)}, s32[1,4096]{1,0:T(1,128)}) custom-call(s32[1,4096]{1,0:T(1,128)} %bitcast.3, s32[1,4096]{1,0:T(1,128)} %bitcast.5, f32[4096,128]{1,0:T(8,128)} %feature_ref.1), custom_call_target="tpu_custom_call" | custom-call | tf_op jit(solution)/shard_map/local/pallas_call | solution.py:407
  45.0 28.5 %exchange.1 = (bf16[1024,256]{1,0:T(8,128)(2,1)}, f32[1,1024]{1,0:T(1,128)}) custom-call(f32[2,4,136,128]{3,2,1,0:T(8,128)} %get-tuple-element.14.state_ref), custom_call_target="tpu_custom_call" | custom-call | tf_op jit(solution)/shard_map/exchange/pallas_call | solution.py:433
  73.5 9.2 %means.1 = f32[4096,128]{1,0:T(8,128)} custom-call(s32[1,4096]{1,0:T(1,128)} %get-tuple-element.11.open_ref, f32[1,4096]{1,0:T(1,128)} %get-tuple-element.12.own_ref, f32[4096,128]{1,0:T(8,128)} %get-tuple-element.13.sum_ref, bf16[1024,256]{1,0:T(8,128)(2,1)} %get-tuple-element.15.table_ref, f32[1,1024]{1,0:T(1,128)} %get-tuple-element.16.count_ref), custom_call_target="tpu_custom_call" | custom-call | tf_op jit(solution)/shard_map/means/pallas_call | solution.py:454

commit v2 on v1

v2 whole, which is shorter than its diff:
```python
import functools
import math

import jax
import jax.numpy as jnp
from jax import lax
from jax.experimental import pallas as pl
from jax.experimental.pallas import tpu as pltpu
from jax.sharding import PartitionSpec as P

ACCOUNTS = 128
LANES = 128
TILE = ACCOUNTS + 8
VMEM_LIMIT = 60 * 1024 * 1024


def column_of(row):
    return jnp.transpose(jnp.broadcast_to(row, (LANES, LANES)))


def row_of(column):
    return jnp.transpose(column)[0:1, :]


def lane_ids(first):
    return lax.broadcasted_iota(jnp.int32, (1, LANES), 1) + first


def lane_slice(start):
    return pl.ds(pl.multiple_of(start, LANES), LANES)


def split_store(ref, rows, values):
    high = values.astype(jnp.bfloat16)
    ref[rows, 0:LANES] = high
    ref[rows, LANES : 2 * LANES] = (values - high.astype(jnp.float32)).astype(jnp.bfloat16)


def stacked(rows16):
    return jnp.concatenate([rows16] * (LANES // 16), axis=0)


def short(values):
    return values.astype(jnp.int16)


def one_if(condition):
    return jnp.where(condition, jnp.bfloat16(1), jnp.bfloat16(0))


def prepare(home_ref, account_ref, flag_ref, feature_ref, halves_ref, user_ref, user16_ref, flagged16_ref, pos16_ref):
    chunks = feature_ref.shape[0] // LANES
    step = math.gcd(chunks, 4)

    @pl.loop(0, chunks // step)
    def _(trip):
        for inner in range(step):
            chunk = trip * step + inner
            at = lane_slice(chunk * LANES)
            pos = lane_ids(chunk * LANES + 1)
            user = home_ref[0:1, at] * ACCOUNTS + account_ref[0:1, at]
            flagged = jnp.where(flag_ref[0:1, at] > 0, user, -1)
            user_ref[0:1, at] = user
            user16_ref[:, at] = short(jnp.broadcast_to(user, (16, LANES)))
            flagged16_ref[:, at] = short(jnp.broadcast_to(flagged, (16, LANES)))
            pos16_ref[:, at] = short(jnp.broadcast_to(pos, (16, LANES)))
            split_store(halves_ref, at, feature_ref[at, :])


def row_max(found):
    return jnp.max(jnp.transpose(found.astype(jnp.int32)), axis=0, keepdims=True)


def row_sum(values):
    return jnp.sum(jnp.transpose(values.astype(jnp.float32)), axis=0, keepdims=True)


def closing_states(halves_ref, user16_ref, flagged16_ref, pos16_ref, state_ref, mask_ref, last_ref):
    events = halves_ref.shape[0]
    chunks = events // LANES
    group = mask_ref.shape[0]
    parts = group // ACCOUNTS
    users = state_ref.shape[1] * 2 * ACCOUNTS
    step = math.gcd(chunks, 8)

    @pl.loop(0, users // group)
    def _(block):
        def ids_of(part):
            return short(
                lax.broadcasted_iota(jnp.int32, (ACCOUNTS, LANES), 0)
                + (block * parts + part) * ACCOUNTS
            )

        def latest(trip, found):
            for inner in range(step):
                at = lane_slice((trip * step + inner) * LANES)
                flagged, pos = stacked(flagged16_ref[:, at]), stacked(pos16_ref[:, at])
                found = tuple(
                    jnp.where(flagged == ids_of(part), pos, found[part]) for part in range(parts)
                )
            return found

        found = lax.fori_loop(
            0, chunks // step, latest, (jnp.zeros((ACCOUNTS, LANES), jnp.int16),) * parts
        )
        marks = []
        for part in range(parts):
            last = row_max(found[part])
            marks.append(jnp.where(last > 0, 1.0, 0.0))
            last_ref[part * LANES : (part + 1) * LANES, :] = short(column_of(last))

        def build(trip, count):
            for inner in range(step):
                at = lane_slice((trip * step + inner) * LANES)
                user, pos = stacked(user16_ref[:, at]), stacked(pos16_ref[:, at])
                grown = []
                for part in range(parts):
                    here = slice(part * LANES, (part + 1) * LANES)
                    weight = one_if((user == ids_of(part)) & (pos >= last_ref[here, :]))
                    mask_ref[here, at] = weight
                    grown.append(count[part] + weight)
                count = tuple(grown)
            return count

        count = lax.fori_loop(
            0, chunks // step, build, (jnp.zeros((ACCOUNTS, LANES), jnp.bfloat16),) * parts
        )
        total = jnp.dot(mask_ref[...], halves_ref[...], preferred_element_type=jnp.float32)
        total = total[:, 0:LANES] + total[:, LANES : 2 * LANES]
        for part in range(parts):
            owner = block * parts + part
            half, at = lax.rem(owner, 2), owner // 2
            state_ref[half, at, ACCOUNTS:TILE, :] = jnp.concatenate(
                [row_sum(count[part]), marks[part], jnp.zeros((6, LANES), jnp.float32)], axis=0
            )
            state_ref[half, at, 0:ACCOUNTS, :] = total[part * ACCOUNTS : (part + 1) * ACCOUNTS]


def inside_sessions(
    first_block, end_block, halves_ref, user_ref, flagged16_ref, pos16_ref,
    sum_ref, count_ref, open_ref, key16_ref, mask_ref, keycol_ref, cnt_ref, acc_ref
):
    rows = acc_ref.shape[0]
    parts = rows // LANES
    diagonal = short(lax.broadcasted_iota(jnp.int32, (LANES, LANES), 1)) <= short(
        lax.broadcasted_iota(jnp.int32, (LANES, LANES), 0)
    )

    @pl.loop(first_block, end_block)
    def _(block):
        base = block * rows
        here = [slice(part * LANES, (part + 1) * LANES) for part in range(parts)]
        mine = [lane_slice(base + part * LANES) for part in range(parts)]
        for part in range(parts):
            keycol_ref[here[part], :] = short(column_of(user_ref[0:1, mine[part]]))

        def latest(trip, found):
            for inner in range(parts):
                at = lane_slice(trip * rows + inner * LANES)
                flagged, pos = stacked(flagged16_ref[:, at]), stacked(pos16_ref[:, at])
                found = tuple(
                    jnp.where(flagged == keycol_ref[here[part], :], pos, found[part])
                    for part in range(parts)
                )
            return found

        found = lax.fori_loop(
            0, block, latest, (jnp.zeros((LANES, LANES), jnp.int16),) * parts
        )
        keys = []
        for part in range(parts):
            seen = found[part]
            for inner in range(part + 1):
                same = stacked(flagged16_ref[:, mine[inner]]) == keycol_ref[here[part], :]
                if inner == part:
                    same = same & diagonal
                seen = jnp.where(same, stacked(pos16_ref[:, mine[inner]]), seen)
            start = row_max(seen)
            user = user_ref[0:1, mine[part]]
            key = jnp.where(start > 0, start, -1 - user)
            keys.append(key)
            open_ref[0:1, mine[part]] = jnp.where(start > 0, -1, user)
        for part in range(parts):
            keycol_ref[here[part], :] = short(column_of(keys[part]))
            key16_ref[:, mine[part]] = short(jnp.broadcast_to(keys[part], (16, LANES)))

        for part in range(parts):
            key = keycol_ref[here[part], :]
            count = jnp.zeros((LANES, LANES), jnp.bfloat16)
            for inner in range(parts):
                if inner > part:
                    mask_ref[here[part], here[inner]] = jnp.zeros((LANES, LANES), jnp.bfloat16)
                    continue
                same = stacked(key16_ref[:, mine[inner]]) == key
                if inner == part:
                    same = same & diagonal
                weight = one_if(same)
                mask_ref[here[part], here[inner]] = weight
                count = count + weight
            cnt_ref[here[part], :] = count
        acc_ref[...] = jnp.dot(
            mask_ref[0:rows, 0:rows],
            halves_ref[pl.ds(pl.multiple_of(base, rows), rows), :],
            preferred_element_type=jnp.float32,
        )

        @pl.loop(0, block)
        def _(trip):
            for part in range(parts):
                key = keycol_ref[here[part], :]
                count = cnt_ref[here[part], :]
                for inner in range(parts):
                    at = lane_slice(trip * rows + inner * LANES)
                    weight = one_if(stacked(key16_ref[:, at]) == key)
                    mask_ref[here[part], here[inner]] = weight
                    count = count + weight
                cnt_ref[here[part], :] = count
            acc_ref[...] += jnp.dot(
                mask_ref[0:rows, 0:rows],
                halves_ref[pl.ds(pl.multiple_of(trip * rows, rows), rows), :],
                preferred_element_type=jnp.float32,
            )

        sum_ref[pl.ds(pl.multiple_of(base, rows), rows), :] = (
            acc_ref[:, 0:LANES] + acc_ref[:, LANES : 2 * LANES]
        )
        for part in range(parts):
            count_ref[0:1, mine[part]] = row_sum(cnt_ref[here[part], :])


def sums_of(tile):
    return tile[0:ACCOUNTS, :]


def stats_of(tile):
    return tile[ACCOUNTS:TILE, :]


def follow(earlier, later):
    stats_e, stats_l = stats_of(earlier), stats_of(later)
    mark = stats_l[1:2, :]
    carry_on = 1.0 - mark
    sums = sums_of(later) + column_of(carry_on) * sums_of(earlier)
    count = stats_l[0:1, :] + carry_on * stats_e[0:1, :]
    seen = jnp.maximum(mark, stats_e[1:2, :])
    return jnp.concatenate([sums, count, seen, stats_l[2:8, :]], axis=0)


def exchange(
    groups, owners, home_ref, account_ref, flag_ref, feature_ref,
    table_ref, count_ref, sum_ref, own_count_ref, open_ref,
    state_ref, halves, user_ref, user16, flagged16, pos16, key16, mask, last, keycol, cnt, acc,
    pair_in, chip, chip_in, time_out, time_in, back_out, back_in, pair_out, pair_back, sends, recvs,
):
    chips = owners // 2
    time, me = lax.axis_index("tm"), lax.axis_index("users")
    core, z = lax.rem(me, 2), me // 2
    sibling = me + 1 - 2 * core
    other = 1 - core
    zeros = jnp.zeros((TILE, LANES), jnp.float32)

    def copy(source, target, stage, mine, theirs, device):
        return pltpu.make_async_remote_copy(
            src_ref=source,
            dst_ref=target,
            send_sem=sends.at[stage, mine],
            recv_sem=recvs.at[stage, theirs],
            device_id=device,
            device_id_type=pl.DeviceIdType.MESH,
        )

    def peer(shift):
        return lax.rem(z + shift, chips)

    def each(first, last, fn):
        if last - first <= 8:
            for index in range(first, last):
                fn(index)
        else:
            pl.loop(first, last)(fn)

    def device(group, user):
        return (group, user)

    barrier = pltpu.get_barrier_semaphore()
    pl.semaphore_signal(barrier, inc=1, device_id=device(time, sibling), device_id_type=pl.DeviceIdType.MESH)
    each(1, chips, lambda k: pl.semaphore_signal(
        barrier, inc=1, device_id=device(time, 2 * peer(k) + core), device_id_type=pl.DeviceIdType.MESH))
    each(1, groups, lambda k: pl.semaphore_signal(
        barrier, inc=1, device_id=device(lax.rem(time + k, groups), me), device_id_type=pl.DeviceIdType.MESH))

    prepare(home_ref, account_ref, flag_ref, feature_ref, halves, user_ref, user16, flagged16, pos16)
    closing_states(halves, user16, flagged16, pos16, state_ref, mask, last)
    blocks = sum_ref.shape[0] // acc.shape[0]
    early = blocks * 5 // 8

    def inside(first, end):
        inside_sessions(first, end, halves, user_ref, flagged16, pos16,
                        sum_ref, own_count_ref, open_ref, key16, mask, keycol, cnt, acc)

    pl.semaphore_wait(barrier, 1 + (chips - 1) + (groups - 1))

    def swap(k):
        to = peer(k)
        copy(state_ref.at[other, to], pair_in.at[to], 0, to, to, device(time, sibling)).start()

    each(1, chips, swap)
    swap(0)

    def gather(k):
        to = peer(k)
        got = copy(state_ref.at[other, to], pair_in.at[to], 0, to, to, device(time, sibling))
        got.wait_recv()
        mine, theirs = state_ref[core, to], pair_in[to]
        first = core == 0
        chip[to] = follow(jnp.where(first, mine, theirs), jnp.where(first, theirs, mine))

    def to_owner(k):
        to = peer(k)
        return copy(chip.at[to], chip_in.at[z], 1, to, z, device(time, 2 * to + core))

    def gather_send(k):
        gather(k)
        to_owner(k).start()

    each(1, chips, gather_send)
    gather(0)
    chip_in[z] = chip[z]
    inside(0, early)

    def from_owner(k):
        source = peer(k)
        copy(chip.at[source], chip_in.at[source], 1, source, source, device(time, 2 * source + core)).wait_recv()

    each(1, chips, from_owner)

    total = lax.fori_loop(0, chips, lambda at, so_far: follow(so_far, chip_in[at]), zeros)
    time_out[...] = total

    def to_time(k):
        to = lax.rem(time + k, groups)
        return copy(time_out, time_in.at[time], 2, to, time, device(to, me))

    each(1, groups, lambda k: to_time(k).start())
    time_in[time] = zeros

    def from_time(k):
        source = lax.rem(time + k, groups)
        copy(time_out, time_in.at[source], 2, source, source, device(source, me)).wait_recv()

    each(1, groups, from_time)

    def advance(at, so_far):
        return jnp.where(at < time, follow(so_far, time_in[at]), so_far)

    incoming = lax.fori_loop(0, groups, advance, zeros)

    def prefixes(at, so_far):
        back_out[at] = so_far
        return follow(so_far, chip_in[at])

    lax.fori_loop(0, chips, prefixes, incoming)

    def to_chip(k):
        to = peer(k)
        return copy(back_out.at[to], back_in.at[z], 3, to, z, device(time, 2 * to + core))

    each(1, chips, lambda k: to_chip(k).start())
    back_in[z] = back_out[z]
    inside(early, blocks)

    def finish(half, at, tile):
        owner = 2 * at + half
        split_store(table_ref, lane_slice(owner * ACCOUNTS), sums_of(tile))
        count_ref[0:1, lane_slice(owner * ACCOUNTS)] = stats_of(tile)[0:1, :]

    def to_sibling(at):
        return copy(pair_out.at[at], pair_back.at[at], 4, at, at, device(time, sibling))

    def hand_over(k):
        at = peer(k)
        tile = back_in[at]
        first = core == 0
        after = follow(tile, jnp.where(first, state_ref[core, at], pair_in[at]))
        pair_out[at] = jnp.where(first, after, tile)
        to_sibling(at).start()
        finish(core, at, jnp.where(first, tile, after))

    def wait_hand_over(k):
        source = peer(k)
        copy(back_out.at[source], back_in.at[source], 3, source, source, device(time, 2 * source + core)).wait_recv()
        hand_over(k)

    hand_over(0)
    each(1, chips, wait_hand_over)

    def last(k):
        at = peer(k)
        to_sibling(at).wait_recv()
        finish(other, at, pair_back[at])

    each(0, chips, last)

    def drain(k):
        to = peer(k)
        to_owner(k).wait_send()
        to_chip(k).wait_send()

    def drain_pair(k):
        to = peer(k)
        copy(state_ref.at[other, to], pair_in.at[to], 0, to, to, device(time, sibling)).wait_send()
        to_sibling(to).wait_send()

    each(1, chips, drain)
    each(0, chips, drain_pair)
    each(1, groups, lambda k: to_time(k).wait_send())


def means(open_ref, own_ref, sum_ref, table_ref, count_ref, out_ref, mask_ref):
    rows, users = mask_ref.shape
    high = (count_ref[...] * (1.0 / 32768.0)).astype(jnp.int32)
    low = count_ref[...].astype(jnp.int32) - high * 32768
    counts = []
    for part in range(rows // LANES):
        here = slice(part * LANES, (part + 1) * LANES)
        ids = short(column_of(open_ref[0:1, here]))

        def build(chunk, found, rows_of):
            at = lane_slice(chunk * LANES)
            same = short(jnp.broadcast_to(lane_ids(chunk * LANES), (LANES, LANES))) == ids
            mask_ref[here, at] = one_if(same)
            return tuple(
                jnp.where(same, short(jnp.broadcast_to(row, (LANES, LANES))), so_far)
                for row, so_far in zip(rows_of(chunk), found)
            )

        found = (jnp.zeros((LANES, LANES), jnp.int16),) * 2
        if users <= 1024:
            for chunk in range(users // LANES):
                at = slice(chunk * LANES, (chunk + 1) * LANES)
                found = build(chunk, found, lambda chunk: (high[:, at], low[:, at]))
        else:
            def pieces(chunk):
                count = count_ref[0:1, lane_slice(chunk * LANES)]
                upper = (count * (1.0 / 32768.0)).astype(jnp.int32)
                return upper, count.astype(jnp.int32) - upper * 32768

            found = lax.fori_loop(
                0, users // LANES, lambda chunk, found: build(chunk, found, pieces), found
            )
        count = found[0].astype(jnp.int32) * 32768 + found[1].astype(jnp.int32)
        counts.append(row_sum(count) + own_ref[0:1, here])
    before = jnp.dot(mask_ref[...], table_ref[...], preferred_element_type=jnp.float32)
    before = before[:, 0:LANES] + before[:, LANES : 2 * LANES]
    for part in range(rows // LANES):
        here = slice(part * LANES, (part + 1) * LANES)
        out_ref[here, :] = (sum_ref[here, :] + before[here]) / column_of(counts[part])


def body(groups, owners, features, home, account, flags):
    events = features.shape[0]
    users = owners * ACCOUNTS
    chips = owners // 2
    rows = math.gcd(events, 512)
    group = math.gcd(users, 512)
    whole = pl.BlockSpec(memory_space=pltpu.VMEM)
    tiles = lambda *count: pltpu.VMEM((*count, TILE, LANES), jnp.float32)
    lots = max(chips, groups)
    table, prefix_count, own_sum, own_count, open_user = pl.pallas_call(
        functools.partial(exchange, groups, owners),
        out_shape=(
            jax.ShapeDtypeStruct((users, 2 * LANES), jnp.bfloat16),
            jax.ShapeDtypeStruct((1, users), jnp.float32),
            jax.ShapeDtypeStruct((events, LANES), jnp.float32),
            jax.ShapeDtypeStruct((1, events), jnp.float32),
            jax.ShapeDtypeStruct((1, events), jnp.int32),
        ),
        in_specs=[whole] * 4,
        out_specs=(whole,) * 5,
        scratch_shapes=[
            tiles(2, chips),
            pltpu.VMEM((events, 2 * LANES), jnp.bfloat16),
            pltpu.VMEM((1, events), jnp.int32),
            pltpu.VMEM((16, events), jnp.int16),
            pltpu.VMEM((16, events), jnp.int16),
            pltpu.VMEM((16, events), jnp.int16),
            pltpu.VMEM((16, events), jnp.int16),
            pltpu.VMEM((group, events), jnp.bfloat16),
            pltpu.VMEM((group, LANES), jnp.int16),
            pltpu.VMEM((rows, LANES), jnp.int16),
            pltpu.VMEM((rows, LANES), jnp.bfloat16),
            pltpu.VMEM((rows, 2 * LANES), jnp.float32),
            tiles(chips), tiles(chips), tiles(chips),
            tiles(), tiles(groups),
            tiles(chips), tiles(chips), tiles(chips), tiles(chips),
            pltpu.SemaphoreType.DMA((5, lots)),
            pltpu.SemaphoreType.DMA((5, lots)),
        ],
        compiler_params=pltpu.CompilerParams(
            collective_id=0, has_side_effects=True, vmem_limit_bytes=VMEM_LIMIT
        ),
        name="exchange",
    )(home.reshape(1, events), account.reshape(1, events), flags.reshape(1, events), features)

    return pl.pallas_call(
        means,
        grid=(events // rows,),
        out_shape=jax.ShapeDtypeStruct((events, LANES), jnp.float32),
        in_specs=[
            pl.BlockSpec((1, rows), lambda i: (0, i)),
            pl.BlockSpec((1, rows), lambda i: (0, i)),
            pl.BlockSpec((rows, LANES), lambda i: (i, 0)),
            pl.BlockSpec((users, 2 * LANES), lambda i: (0, 0)),
            pl.BlockSpec((1, users), lambda i: (0, 0)),
        ],
        out_specs=pl.BlockSpec((rows, LANES), lambda i: (i, 0)),
        scratch_shapes=[pltpu.VMEM((rows, users), jnp.bfloat16)],
        compiler_params=pltpu.CompilerParams(vmem_limit_bytes=VMEM_LIMIT),
        name="means",
    )(open_user, own_count, own_sum, table, prefix_count)


def solution(mesh):
    return jax.shard_map(
        functools.partial(body, mesh.shape["tm"], mesh.shape["users"]),
        mesh=mesh,
        in_specs=(
            P(("tm", "users"), None),
            P(("tm", "users"), None),
            P(("tm", "users")),
            P(("tm", "users")),
        ),
        out_specs=P(("tm", "users"), None),
        check_vma=False,
    )
```

time: 83.1 us -> 49.4 us (0.59)
  Pallas kernels: 80.6 us -> 49.1 us
  other arithmetic: 2.05 us -> 0 us
    pallas_call x1 -> x0, Pallas kernels: 42.9 us -> none  [body(): pl.pallas_call(local_kernel, out_shape=(jax.ShapeDtypeStruct((2, chips, T...]
    pallas_call x1, Pallas kernels: 28.5 us -> 40.6 us  [body(): pl.pallas_call(functools.partial(exchange, groups, owners), out_shape=(ja...]
    add x1 -> x0, other arithmetic: 1.32 us -> none  [body(): user = home.reshape(1, events) * ACCOUNTS + account.reshape(1, events)]
where the time goes in v2:
time: 49.4 us; the launch traced here: 49.1 us
  Pallas kernels  49.1 us (99%)
    pallas_call x1, Pallas kernels, body(): pl.pallas_call(functools.partial(exchange, groups, owners), out_shape=(ja...  40.6 us
    pallas_call x1, Pallas kernels, body(): pl.pallas_call(means, grid=(events // rows,), out_shape=jax.ShapeDtypeStr...  8.43 us

profile of v2, /device:TPU:0, one launch (start us, length us, event | category | flops | bytes accessed | tf_op | source)
XLA Modules:
  0.0 49.1 jit_solution(16551857724726051212)
XLA Ops:
  0.0 40.6 %exchange.1 = (bf16[1024,256]{1,0:T(8,128)(2,1)}, f32[1,1024]{1,0:T(1,128)}, f32[4096,128]{1,0:T(8,128)}, f32[1,4096]{1,0:T(1,128)}, s32[1,4096]{1,0:T(1,128)}) custom-call(s32[1,4096]{1,0:T(1,128)} %bitcast.3, s32[1,4096]{1,0:T(1,128)} %bitcast.4, s32[1,4096]{1,0:T(1,128)} %bitcast.5, f32[4096,128]{1,0:T(8,128)} %feature_ref.1), custom_call_target="tpu_custom_call" | custom-call | tf_op jit(solution)/shard_map/exchange/pallas_call | solution.py:469
  40.6 8.4 %means.1 = f32[4096,128]{1,0:T(8,128)} custom-call(s32[1,4096]{1,0:T(1,128)} %get-tuple-element.10.open_ref, f32[1,4096]{1,0:T(1,128)} %get-tuple-element.11.own_ref, f32[4096,128]{1,0:T(8,128)} %get-tuple-element.12.sum_ref, bf16[1024,256]{1,0:T(8,128)(2,1)} %get-tuple-element.13.table_ref, f32[1,1024]{1,0:T(1,128)} %get-tuple-element.14.count_ref), custom_call_target="tpu_custom_call" | custom-call | tf_op jit(solution)/shard_map/means/pallas_call | solution.py:505

commit v3 on v2

--- a/solution.py
+++ b/solution.py
@@ -130,10 +130,10 @@
         for part in range(parts):
             owner = block * parts + part
             half, at = lax.rem(owner, 2), owner // 2
-            state_ref[half, at, ACCOUNTS:TILE, :] = jnp.concatenate(
+            state_ref[half, at, 0:8, :] = jnp.concatenate(
                 [row_sum(count[part]), marks[part], jnp.zeros((6, LANES), jnp.float32)], axis=0
             )
-            state_ref[half, at, 0:ACCOUNTS, :] = total[part * ACCOUNTS : (part + 1) * ACCOUNTS]
+            state_ref[half, at, 8:TILE, :] = total[part * ACCOUNTS : (part + 1) * ACCOUNTS]
 
 
 def inside_sessions(
@@ -228,22 +228,19 @@
             count_ref[0:1, mine[part]] = row_sum(cnt_ref[here[part], :])
 
 
-def sums_of(tile):
-    return tile[0:ACCOUNTS, :]
-
-
-def stats_of(tile):
-    return tile[ACCOUNTS:TILE, :]
-
-
-def follow(earlier, later):
-    stats_e, stats_l = stats_of(earlier), stats_of(later)
-    mark = stats_l[1:2, :]
+SPANS = ((0, 8 + ACCOUNTS // 2), (8 + ACCOUNTS // 2, TILE))
+
+
+def follow(earlier, later, stats, part):
+    mark = stats[1:2, :]
     carry_on = 1.0 - mark
-    sums = sums_of(later) + column_of(carry_on) * sums_of(earlier)
-    count = stats_l[0:1, :] + carry_on * stats_e[0:1, :]
-    seen = jnp.maximum(mark, stats_e[1:2, :])
-    return jnp.concatenate([sums, count, seen, stats_l[2:8, :]], axis=0)
+    column = column_of(carry_on)
+    if part:
+        return later + column[ACCOUNTS // 2 :] * earlier
+    sums = later[8:] + column[0 : ACCOUNTS // 2] * earlier[8:]
+    count = later[0:1] + carry_on * earlier[0:1]
+    seen = jnp.maximum(mark, earlier[1:2])
+    return jnp.concatenate([count, seen, later[2:8], sums], axis=0)
 
 
 def exchange(
@@ -257,14 +254,28 @@
     core, z = lax.rem(me, 2), me // 2
     sibling = me + 1 - 2 * core
     other = 1 - core
-    zeros = jnp.zeros((TILE, LANES), jnp.float32)
-
-    def copy(source, target, stage, mine, theirs, device):
+
+    def cut(ref, part, *at):
+        return ref.at[(*at, pl.ds(SPANS[part][0], SPANS[part][1] - SPANS[part][0]))]
+
+    def get(ref, part, *at):
+        return ref[(*at, slice(*SPANS[part]), slice(None))]
+
+    def put(ref, part, values, *at):
+        ref[(*at, slice(*SPANS[part]), slice(None))] = values
+
+    def stats(ref, *at):
+        return ref[(*at, slice(0, 8), slice(None))]
+
+    def empty(part):
+        return jnp.zeros((SPANS[part][1] - SPANS[part][0], LANES), jnp.float32)
+
+    def copy(source, target, stage, part, mine, theirs, device):
         return pltpu.make_async_remote_copy(
             src_ref=source,
             dst_ref=target,
-            send_sem=sends.at[stage, mine],
-            recv_sem=recvs.at[stage, theirs],
+            send_sem=sends.at[2 * stage + part, mine],
+            recv_sem=recvs.at[2 * stage + part, theirs],
             device_id=device,
             device_id_type=pl.DeviceIdType.MESH,
         )
@@ -292,7 +303,6 @@
     prepare(home_ref, account_ref, flag_ref, feature_ref, halves, user_ref, user16, flagged16, pos16)
     closing_states(halves, user16, flagged16, pos16, state_ref, mask, last)
     blocks = sum_ref.shape[0] // acc.shape[0]
-    early = blocks * 5 // 8
 
     def inside(first, end):
         inside_sessions(first, end, halves, user_ref, flagged16, pos16,
@@ -300,120 +310,129 @@
 
     pl.semaphore_wait(barrier, 1 + (chips - 1) + (groups - 1))
 
-    def swap(k):
-        to = peer(k)
-        copy(state_ref.at[other, to], pair_in.at[to], 0, to, to, device(time, sibling)).start()
-
-    each(1, chips, swap)
-    swap(0)
-
-    def gather(k):
-        to = peer(k)
-        got = copy(state_ref.at[other, to], pair_in.at[to], 0, to, to, device(time, sibling))
-        got.wait_recv()
-        mine, theirs = state_ref[core, to], pair_in[to]
-        first = core == 0
-        chip[to] = follow(jnp.where(first, mine, theirs), jnp.where(first, theirs, mine))
-
-    def to_owner(k):
-        to = peer(k)
-        return copy(chip.at[to], chip_in.at[z], 1, to, z, device(time, 2 * to + core))
-
-    def gather_send(k):
-        gather(k)
-        to_owner(k).start()
-
-    each(1, chips, gather_send)
-    gather(0)
-    chip_in[z] = chip[z]
-    inside(0, early)
-
-    def from_owner(k):
-        source = peer(k)
-        copy(chip.at[source], chip_in.at[source], 1, source, source, device(time, 2 * source + core)).wait_recv()
-
-    each(1, chips, from_owner)
-
-    total = lax.fori_loop(0, chips, lambda at, so_far: follow(so_far, chip_in[at]), zeros)
-    time_out[...] = total
-
-    def to_time(k):
+    first = core == 0
+    shares = [blocks * n // 8 for n in (4, 5, 6)]
+
+    def pair_copy(part, to):
+        return copy(cut(state_ref, part, other, to), cut(pair_in, part, to), 0, part, to, to, device(time, sibling))
+
+    for part in (0, 1):
+        each(1, chips, lambda k: pair_copy(part, peer(k)).start())
+        pair_copy(part, z).start()
+
+    def to_owner(part, to):
+        return copy(cut(chip, part, to), cut(chip_in, part, z), 1, part, to, z, device(time, 2 * to + core))
+
+    def gather(part, to):
+        pair_copy(part, to).wait_recv()
+        mine, theirs = get(state_ref, part, core, to), get(pair_in, part, to)
+        later = jnp.where(first, stats(pair_in, to), stats(state_ref, core, to))
+        return follow(jnp.where(first, mine, theirs), jnp.where(first, theirs, mine), later, part)
+
+    for part in (0, 1):
+        def gather_send(k):
+            to = peer(k)
+            put(chip, part, gather(part, to), to)
+            to_owner(part, to).start()
+
+        each(1, chips, gather_send)
+    for part in (0, 1):
+        put(chip_in, part, gather(part, z), z)
+    inside(0, shares[0])
+
+    def to_time(part, k):
         to = lax.rem(time + k, groups)
-        return copy(time_out, time_in.at[time], 2, to, time, device(to, me))
-
-    each(1, groups, lambda k: to_time(k).start())
-    time_in[time] = zeros
-
-    def from_time(k):
-        source = lax.rem(time + k, groups)
-        copy(time_out, time_in.at[source], 2, source, source, device(source, me)).wait_recv()
-
-    each(1, groups, from_time)
-
-    def advance(at, so_far):
-        return jnp.where(at < time, follow(so_far, time_in[at]), so_far)
-
-    incoming = lax.fori_loop(0, groups, advance, zeros)
-
-    def prefixes(at, so_far):
-        back_out[at] = so_far
-        return follow(so_far, chip_in[at])
-
-    lax.fori_loop(0, chips, prefixes, incoming)
-
-    def to_chip(k):
-        to = peer(k)
-        return copy(back_out.at[to], back_in.at[z], 3, to, z, device(time, 2 * to + core))
-
-    each(1, chips, lambda k: to_chip(k).start())
-    back_in[z] = back_out[z]
-    inside(early, blocks)
-
-    def finish(half, at, tile):
+        return copy(cut(time_out, part), cut(time_in, part, time), 2, part, to, time, device(to, me))
+
+    for part in (0, 1):
+        def from_owner(k):
+            source = peer(k)
+            copy(cut(chip, part, source), cut(chip_in, part, source), 1, part, source, source,
+                 device(time, 2 * source + core)).wait_recv()
+
+        each(1, chips, from_owner)
+        put(time_out, part, lax.fori_loop(
+            0, chips,
+            lambda at, so_far: follow(so_far, get(chip_in, part, at), stats(chip_in, at), part),
+            empty(part), unroll=chips <= 8))
+        each(1, groups, lambda k: to_time(part, k).start())
+        put(time_in, part, empty(part), time)
+        inside(shares[part], shares[part + 1])
+
+    def to_chip(part, to):
+        return copy(cut(back_out, part, to), cut(back_in, part, z), 3, part, to, z, device(time, 2 * to + core))
+
+    for part in (0, 1):
+        def from_time(k):
+            source = lax.rem(time + k, groups)
+            copy(cut(time_out, part), cut(time_in, part, source), 2, part, source, source,
+                 device(source, me)).wait_recv()
+
+        each(1, groups, from_time)
+
+        def advance(at, so_far):
+            after = follow(so_far, get(time_in, part, at), stats(time_in, at), part)
+            return jnp.where(at < time, after, so_far)
+
+        def prefixes(at, so_far):
+            put(back_out, part, so_far, at)
+            return follow(so_far, get(chip_in, part, at), stats(chip_in, at), part)
+
+        incoming = lax.fori_loop(0, groups, advance, empty(part), unroll=True)
+        lax.fori_loop(0, chips, prefixes, incoming, unroll=chips <= 8)
+        each(1, chips, lambda k: to_chip(part, peer(k)).start())
+        put(back_in, part, get(back_out, part, z), z)
+    inside(shares[2], blocks)
+
+    def finish(half, part, at, tile):
         owner = 2 * at + half
-        split_store(table_ref, lane_slice(owner * ACCOUNTS), sums_of(tile))
-        count_ref[0:1, lane_slice(owner * ACCOUNTS)] = stats_of(tile)[0:1, :]
-
-    def to_sibling(at):
-        return copy(pair_out.at[at], pair_back.at[at], 4, at, at, device(time, sibling))
-
-    def hand_over(k):
-        at = peer(k)
-        tile = back_in[at]
-        first = core == 0
-        after = follow(tile, jnp.where(first, state_ref[core, at], pair_in[at]))
-        pair_out[at] = jnp.where(first, after, tile)
-        to_sibling(at).start()
-        finish(core, at, jnp.where(first, tile, after))
-
-    def wait_hand_over(k):
-        source = peer(k)
-        copy(back_out.at[source], back_in.at[source], 3, source, source, device(time, 2 * source + core)).wait_recv()
-        hand_over(k)
-
-    hand_over(0)
-    each(1, chips, wait_hand_over)
-
-    def last(k):
-        at = peer(k)
-        to_sibling(at).wait_recv()
-        finish(other, at, pair_back[at])
-
-    each(0, chips, last)
-
-    def drain(k):
-        to = peer(k)
-        to_owner(k).wait_send()
-        to_chip(k).wait_send()
-
-    def drain_pair(k):
-        to = peer(k)
-        copy(state_ref.at[other, to], pair_in.at[to], 0, to, to, device(time, sibling)).wait_send()
-        to_sibling(to).wait_send()
-
-    each(1, chips, drain)
-    each(0, chips, drain_pair)
-    each(1, groups, lambda k: to_time(k).wait_send())
+        size = ACCOUNTS // 2
+        start = pl.multiple_of(owner * ACCOUNTS + part * size, size)
+        split_store(table_ref, pl.ds(start, size), tile if part else tile[8:])
+        if part == 0:
+            count_ref[0:1, lane_slice(owner * ACCOUNTS)] = tile[0:1]
+
+    def to_sibling(part, at):
+        return copy(cut(pair_out, part, at), cut(pair_back, part, at), 4, part, at, at, device(time, sibling))
+
+    for part in (0, 1):
+        def hand_over(k):
+            at = peer(k)
+            tile = get(back_in, part, at)
+            before = jnp.where(first, get(state_ref, part, core, at), get(pair_in, part, at))
+            marks = jnp.where(first, stats(state_ref, core, at), stats(pair_in, at))
+            after = follow(tile, before, marks, part)
+            put(pair_out, part, jnp.where(first, after, tile), at)
+            to_sibling(part, at).start()
+            finish(core, part, at, jnp.where(first, tile, after))
+
+        def wait_hand_over(k):
+            source = peer(k)
+            copy(cut(back_out, part, source), cut(back_in, part, source), 3, part, source, source,
+                 device(time, 2 * source + core)).wait_recv()
+            hand_over(k)
+
+        hand_over(0)
+        each(1, chips, wait_hand_over)
+
+    for part in (0, 1):
+        def last_tile(k):
+            at = peer(k)
+            to_sibling(part, at).wait_recv()
+            finish(other, part, at, get(pair_back, part, at))
+
+        def drain(k):
+            to_owner(part, peer(k)).wait_send()
+            to_chip(part, peer(k)).wait_send()
+
+        def drain_pair(k):
+            pair_copy(part, peer(k)).wait_send()
+            to_sibling(part, peer(k)).wait_send()
+
+        each(0, chips, last_tile)
+        each(1, chips, drain)
+        each(0, chips, drain_pair)
+        each(1, groups, lambda k: to_time(part, k).wait_send())
 
 
 def means(open_ref, own_ref, sum_ref, table_ref, count_ref, out_ref, mask_ref):
@@ -462,6 +481,7 @@
     users = owners * ACCOUNTS
     chips = owners // 2
     rows = math.gcd(events, 512)
+    tall = math.gcd(events, 1024)
     group = math.gcd(users, 512)
     whole = pl.BlockSpec(memory_space=pltpu.VMEM)
     tiles = lambda *count: pltpu.VMEM((*count, TILE, LANES), jnp.float32)
@@ -493,8 +513,8 @@
             tiles(chips), tiles(chips), tiles(chips),
             tiles(), tiles(groups),
             tiles(chips), tiles(chips), tiles(chips), tiles(chips),
-            pltpu.SemaphoreType.DMA((5, lots)),
-            pltpu.SemaphoreType.DMA((5, lots)),
+            pltpu.SemaphoreType.DMA((10, lots)),
+            pltpu.SemaphoreType.DMA((10, lots)),
         ],
         compiler_params=pltpu.CompilerParams(
             collective_id=0, has_side_effects=True, vmem_limit_bytes=VMEM_LIMIT
@@ -504,17 +524,17 @@
 
     return pl.pallas_call(
         means,
-        grid=(events // rows,),
+        grid=(events // tall,),
         out_shape=jax.ShapeDtypeStruct((events, LANES), jnp.float32),
         in_specs=[
-            pl.BlockSpec((1, rows), lambda i: (0, i)),
-            pl.BlockSpec((1, rows), lambda i: (0, i)),
-            pl.BlockSpec((rows, LANES), lambda i: (i, 0)),
+            pl.BlockSpec((1, tall), lambda i: (0, i)),
+            pl.BlockSpec((1, tall), lambda i: (0, i)),
+            pl.BlockSpec((tall, LANES), lambda i: (i, 0)),
             pl.BlockSpec((users, 2 * LANES), lambda i: (0, 0)),
             pl.BlockSpec((1, users), lambda i: (0, 0)),
         ],
-        out_specs=pl.BlockSpec((rows, LANES), lambda i: (i, 0)),
-        scratch_shapes=[pltpu.VMEM((rows, users), jnp.bfloat16)],
+        out_specs=pl.BlockSpec((tall, LANES), lambda i: (i, 0)),
+        scratch_shapes=[pltpu.VMEM((tall, users), jnp.bfloat16)],
         compiler_params=pltpu.CompilerParams(vmem_limit_bytes=VMEM_LIMIT),
         name="means",
     )(open_user, own_count, own_sum, table, prefix_count)

time: 49.4 us -> 43.9 us (0.89)
  Pallas kernels: 49.1 us -> 43.6 us
    pallas_call x1, Pallas kernels: 40.6 us -> 37.1 us  [body(): pl.pallas_call(functools.partial(exchange, groups, owners), out_shape=(ja...]
    pallas_call x1, Pallas kernels: 8.43 us -> 6.58 us  [body(): pl.pallas_call(means, grid=(events // tall,), out_shape=jax.ShapeDtypeStr...]
where the time goes in v3:
time: 43.9 us; the launch traced here: 43.7 us
  Pallas kernels  43.6 us (99%)
    pallas_call x1, Pallas kernels, body(): pl.pallas_call(functools.partial(exchange, groups, owners), out_shape=(ja...  37.1 us
    pallas_call x1, Pallas kernels, body(): pl.pallas_call(means, grid=(events // tall,), out_shape=jax.ShapeDtypeStr...  6.58 us

profile of v3, /device:TPU:0, one launch (start us, length us, event | category | flops | bytes accessed | tf_op | source)
XLA Modules:
  0.0 43.7 jit_solution(9923695309704333349)
XLA Ops:
  0.0 37.1 %exchange.1 = (bf16[1024,256]{1,0:T(8,128)(2,1)}, f32[1,1024]{1,0:T(1,128)}, f32[4096,128]{1,0:T(8,128)}, f32[1,4096]{1,0:T(1,128)}, s32[1,4096]{1,0:T(1,128)}) custom-call(s32[1,4096]{1,0:T(1,128)} %bitcast.3, s32[1,4096]{1,0:T(1,128)} %bitcast.4, s32[1,4096]{1,0:T(1,128)} %bitcast.5, f32[4096,128]{1,0:T(8,128)} %feature_ref.1), custom_call_target="tpu_custom_call" | custom-call | tf_op jit(solution)/shard_map/exchange/pallas_call | solution.py:489
  37.1 6.6 %means.1 = f32[4096,128]{1,0:T(8,128)} custom-call(s32[1,4096]{1,0:T(1,128)} %get-tuple-element.10.open_ref, f32[1,4096]{1,0:T(1,128)} %get-tuple-element.11.own_ref, f32[4096,128]{1,0:T(8,128)} %get-tuple-element.12.sum_ref, bf16[1024,256]{1,0:T(8,128)(2,1)} %get-tuple-element.13.table_ref, f32[1,1024]{1,0:T(1,128)} %get-tuple-element.14.count_ref), custom_call_target="tpu_custom_call" | custom-call | tf_op jit(solution)/shard_map/means/pallas_call | solution.py:525
